TPU v7x, 256 devices: a whole 4x4x8 slice. The times are simulated.
256 devices in a mesh: seq: 64 (over z, x, core), head: 4 (over y).
Axes of the slice: x: 4, y: 4, z: 8, core: 2. Of those that a mesh axis runs over, the one named last changes fastest.
Arguments:
- tokens: bfloat16 [65536, 2048], P('seq', 'head'), may hold values from -8 to 8
- w_query: bfloat16 [2048, 2048], P(None, 'head'), may hold values from -1 to 1, as said below
- w_key: bfloat16 [2048, 2048], P(None, 'head'), may hold values from -1 to 1, as said below
- w_value: bfloat16 [2048, 2048], P(None, 'head'), may hold values from -0.125 to 0.125
- w_out: bfloat16 [2048, 2048], P('head'), may hold values from -0.125 to 0.125
- mix_logit: float32 [8], P('head'), may hold values from -2 to 2
Outputs:
- layer_out: bfloat16 [65536, 2048], P('seq', 'head')
Inputs may be any that keep to these rules, and one draw needn't show every extreme that they name: `w_query`: entries of mean zero with a standard deviation of about 2048 ** -0.5. `w_key`: entries of mean zero with a standard deviation of about 2048 ** -0.5.
All inputs are finite; a program needn't handle non-finite values.
Results may differ from a plain program's by a relative error of at most 0.0065.
Values may be sent and summed in bfloat16 or wider, within the bound.
A program may use at most 128 MiB of HBM per device.

v0:
```python
import jax
import jax.numpy as jnp
from jax import lax
from jax.sharding import Mesh
from jax.sharding import PartitionSpec as P

SEQ = ("seq_0", "seq_1", "seq_2")


def nothing_yet(shard, identity):
    return jax.tree.map(
        lambda a, e: jnp.broadcast_to(jnp.asarray(e, a.dtype), a.shape), shard, identity
    )


def carried_in(shard, axes, combine, identity):
    before = start = nothing_yet(shard, identity)
    running = shard
    for axis in reversed(axes):
        length, mine = (lax.axis_size(axis), lax.axis_index(axis))
        pieces = jax.tree.map(
            lambda part, kind: lax.all_gather(part.astype(kind), axis),
            running,
            (jnp.bfloat16, jnp.bfloat16),
        )
        inside, running = (start, start)
        for k in range(length):
            passed = k < mine
            running = combine(
                running, jax.tree.map(lambda part, own: part[k].astype(own.dtype), pieces, shard)
            )
            inside = jax.tree.map(lambda new, old: jnp.where(passed, new, old), running, inside)
        before = combine(inside, before)
    return before


def feature(values):
    return jax.nn.elu(values) + 1.0


def add_pairs(earlier, later):
    return (earlier[0] + later[0], earlier[1] + later[1])


def on_device(tokens, w_query, w_key, w_value, w_out, mix_logit):
    seg = tokens.shape[0]
    heads = mix_logit.shape[0]
    width = w_query.shape[1]
    hsize = width // heads
    empty = jnp.zeros((seg, width), jnp.float32)
    totals = (empty, empty, empty)
    piece = lax.all_gather(tokens, "head", axis=1, tiled=True)
    result = []
    for total, weight in zip(totals, (w_query, w_key, w_value)):
        result.append(jnp.dot(piece, weight, preferred_element_type=jnp.float32))
    query, keys, values = tuple(result)
    query = query.astype(jnp.bfloat16).reshape(seg, heads, hsize)
    keys = keys.astype(jnp.bfloat16).reshape(seg, heads, hsize)
    values = values.astype(jnp.bfloat16).reshape(seg, heads, hsize)
    fkey = feature(keys.astype(jnp.float32)).astype(jnp.bfloat16)
    mem_term = jnp.einsum("thd,the->hde", fkey, values, preferred_element_type=jnp.float32)
    norm_term = jnp.sum(fkey.astype(jnp.float32), axis=0)
    zeros_pair = (jnp.zeros_like(mem_term), jnp.zeros_like(norm_term))
    memory, normal = carried_in((mem_term, norm_term), SEQ, add_pairs, zeros_pair)
    rows = lax.broadcasted_iota(jnp.int32, (seg, seg), 0)
    cols = lax.broadcasted_iota(jnp.int32, (seg, seg), 1)
    causal = cols <= rows
    scale = 1.0 / hsize**0.5
    scores = jnp.einsum("qhd,khd->hqk", query, keys, preferred_element_type=jnp.float32) * scale
    scores = jnp.where(causal[None], scores, -1e30)
    expo = jnp.exp(scores - jnp.max(scores, axis=2, keepdims=True))
    probs = (expo / jnp.sum(expo, axis=2, keepdims=True)).astype(jnp.bfloat16)
    local = jnp.einsum("hqk,khd->qhd", probs, values, preferred_element_type=jnp.float32)
    fquery = feature(query.astype(jnp.float32)).astype(jnp.bfloat16).astype(jnp.float32)
    numer = jnp.einsum("thd,hde->the", fquery, memory, precision=lax.Precision.HIGHEST)
    denom = jnp.einsum("thd,hd->th", fquery, normal, precision=lax.Precision.HIGHEST)
    readout = numer / jnp.maximum(denom, 1.0)[:, :, None]
    share = jax.nn.sigmoid(mix_logit)[None, :, None]
    mixed = (share * readout + (1.0 - share) * local).astype(jnp.bfloat16).reshape(seg, width)
    columns = lax.all_to_all(w_out, "head", split_axis=1, concat_axis=0, tiled=True)
    summed = jnp.dot(
        lax.all_gather(mixed, "head", axis=1, tiled=True),
        columns,
        preferred_element_type=jnp.float32,
    )
    return summed.astype(jnp.bfloat16)


def solution(mesh):
    torus = Mesh(
        mesh.devices.reshape(8, 4, 2, mesh.shape["head"]), ("seq_0", "seq_1", "seq_2", "head")
    )
    return jax.shard_map(
        on_device,
        mesh=torus,
        in_specs=(
            P(SEQ, "head"),
            P(None, "head"),
            P(None, "head"),
            P(None, "head"),
            P("head", None),
            P("head"),
        ),
        out_specs=P(SEQ, "head"),
        check_vma=False,
    )
```

profile of v0, /device:TPU:1, one launch (start us, length us, event | category | flops | bytes accessed | tf_op | source)
XLA Modules:
  0.0 251.1 jit_solution(9462103053753191697)
XLA Ops:
  6.5 0.0 copy-start
  6.5 0.0 all-gather.6.cloned.1.call-start
  6.5 0.7 all-gather.6.cloned.1.call-update
  7.3 0.0 all-gather.8.cloned.1.call-start
  7.3 56.3 %all-gather.6.cloned.1.call-done = bf16[1024,2048]{1,0:T(8,128)(2,1)} async-done(((bf16[1024,512]{1,0:T(8,128)(2,1)}), bf16[1024,2048]{1,0:T(8,128)(2,1)}) %all-gather.6.cloned.1.call-update) | async-done | bytes 4194320 | tf_op jit(solution)/shard_map/all_gather | solution.py:52
  63.6 0.0 copy-done
  63.6 6.2 %fusion.20 = (bf16[512]{0:T(512)(128)(2,1)S(1)}, bf16[1024,512]{0,1:T(8,128)(2,1)}) fusion(bf16[1024,2048]{1,0:T(8,128)(2,1)} %all-gather.6.cloned.1.call-done, bf16[2048,512]{1,0:T(8,128)(2,1)S(1)} %copy-done), kind=kOutput, calls=%fused_computation.36 | convolution fusion | flops 2151677440 | bytes 7341056 | tf_op jit(solution)/shard_map/dot_general | solution.py:55
  69.8 2.3 copy.33
  72.1 0.0 copy-start.1
  72.1 5.3 %convolution_convert_fusion.2 = bf16[1024,512]{0,1:T(8,128)(2,1)S(1)} fusion(bf16[1024,2048]{1,0:T(8,128)(2,1)} %all-gather.6.cloned.1.call-done, bf16[2048,512]{1,0:T(8,128)(2,1)} %param.9), kind=kOutput, calls=%fused_computation.31 | convolution fusion | flops 2148007936 | bytes 7340032 | tf_op jit(solution)/shard_map/dot_general | solution.py:55
  77.4 0.0 copy-start.3
  77.4 0.0 copy-done.1
  77.4 0.0 copy-start.2
  77.4 1.2 convolution_convert_fusion.4
  78.7 0.0 copy-done.3
  78.7 2.7 %all-gather = bf16[4,256,256]{2,1,0:T(8,128)(2,1)S(1)} all-gather(bf16[2,256,256]{2,1,0:T(8,128)(2,1)S(1)} %convolution_convert_fusion.4), channel_id=2, replica_groups=mesh['seq_0'=8,'seq_1'=4,'seq_2'=2,'head'=4] {'seq_2'}, dimensions={0}, use_global_device_ids=true | all-gather | bytes 786432 | tf_op jit(solution)/shard_map/all_gather | solution.py:22
  81.3 0.8 fusion.59
  82.1 0.0 all-gather.8.cloned.1.call-update
  82.1 0.0 all-gather.10.cloned.1.call-start
  82.2 0.0 copy-done.2
  82.2 24.7 %all-gather.8.cloned.1.call-done = bf16[4,2,256,256]{3,2,1,0:T(8,128)(2,1)} async-done(((bf16[1,2,256,256]{3,2,1,0:T(8,128)(2,1)}), bf16[4,2,256,256]{3,2,1,0:T(8,128)(2,1)}) %all-gather.8.cloned.1.call-update) | async-done | bytes 1048592 | tf_op jit(solution)/shard_map/all_gather | solution.py:22
  106.9 2.0 fusion.55
  108.9 0.0 all-gather.10.cloned.1.call-update
  108.9 0.0 all-gather.12.cloned.1.call-start
  109.0 1.3 iota_compare_fusion
  110.3 6.2 %convolution_convert_fusion.1 = bf16[1024,512]{0,1:T(8,128)(2,1)} fusion(bf16[1024,2048]{1,0:T(8,128)(2,1)} %all-gather.6.cloned.1.call-done, bf16[2048,512]{1,0:T(8,128)(2,1)} %param.7), kind=kOutput, calls=%fused_computation.30 | convolution fusion | flops 2148007936 | bytes 7340032 | tf_op jit(solution)/shard_map/dot_general | solution.py:55
  116.5 2.3 copy.36
  118.8 4.2 %all_gather.40 = bf16[2,2,256]{2,1,0:T(2,128)(2,1)S(1)} all-gather(bf16[1,2,256]{2,1,0:T(2,128)(2,1)S(1)} %all_gather.39), channel_id=1, replica_groups=mesh['seq_0'=8,'seq_1'=4,'seq_2'=2,'head'=4] {'seq_2'}, dimensions={0}, use_global_device_ids=true | all-gather | bytes 3072 | tf_op jit(solution)/shard_map/all_gather | solution.py:22
  123.0 6.7 %all_gather.41 = bf16[4,2,256]{2,1,0:T(2,128)(2,1)S(1)} all-gather(bf16[1,2,256]{2,1,0:T(2,128)(2,1)S(1)} %fusion.106), channel_id=1, replica_groups=mesh['seq_0'=8,'seq_1'=4,'seq_2'=2,'head'=4] {'seq_1'}, dimensions={0}, use_global_device_ids=true | all-gather | bytes 5120 | tf_op jit(solution)/shard_map/all_gather | solution.py:22
  129.7 14.9 %all_gather.42 = bf16[8,2,256]{2,1,0:T(2,128)(2,1)S(1)} all-gather(bf16[1,2,256]{2,1,0:T(2,128)(2,1)S(1)} %fusion.105), channel_id=1, replica_groups=mesh['seq_0'=8,'seq_1'=4,'seq_2'=2,'head'=4] {'seq_0'}, dimensions={0}, use_global_device_ids=true | all-gather | bytes 9216 | tf_op jit(solution)/shard_map/all_gather | solution.py:22
  144.6 2.8 %fusion.56 = f32[2,1,1024]{2,1,0:T(1,128)S(1)} fusion(bf16[1024,2,256]{2,0,1:T(8,128)(2,1)} %copy.36, f32[2,256,1]{1,0,2:T(2,128)S(1)} %fusion.94), kind=kOutput, calls=%fused_computation.76 | convolution fusion | flops 9437184 | bytes 1058816 | tf_op jit(solution)/shard_map/thd,hd->th/dot_general | solution.py:76
  147.4 8.4 %fusion.115 = (f32[2,1024]{1,0:T(2,128)S(1)}, f32[2,1024,1024]{1,2,0:T(8,128)}) fusion(pred[1024,1024]{0,1:T(8,128)(4,1)} %iota_compare_fusion, bf16[1024,2,256]{0,2,1:T(8,128)(2,1)} %bitcast.57, bf16[1024,2,256]{0,2,1:T(8,128)(2,1)} %bitcast.54), kind=kOutput, calls=%fused_computation.145 | convolution fusion | flops 1082131456 | bytes 11542528 | tf_op jit(solution)/shard_map/sub | solution.py:71
  155.8 6.3 %fusion.4 = f32[2,256,1024]{2,1,0:T(8,128)} fusion(bf16[1024,2,256]{0,2,1:T(8,128)(2,1)} %bitcast.59, f32[2,1024,1024]{1,2,0:T(8,128)} %get-tuple-element.8, f32[2,1024]{1,0:T(2,128)S(1)} %get-tuple-element.7), kind=kOutput, calls=%fused_computation.14 | convolution fusion | flops 1077936128 | bytes 11542528 | tf_op jit(solution)/shard_map/hqk,khd->qhd/dot_general | solution.py:73
  162.1 0.0 all-gather.10.cloned.1.call-done
  162.1 7.4 %fusion.15 = bf16[1024,2,256]{0,2,1:T(8,128)(2,1)} fusion(f32[2,256,1024]{2,1,0:T(8,128)} %fusion.4, f32[2]{0:T(128)S(1)} %get-tuple-element.5, f32[1024,2]{0,1:T(2,128)S(1)} %fusion.90, f32[2]{0:T(128)S(1)} %get-tuple-element.6, bf16[1024,2,256]{2,0,1:T(8,128)(2,1)} %copy.36, bf16[8,2,256,256]{3,2,1,0:T(8,128)(2,1)} %all-gather.10.cloned.1.call-done, ...), kind=kOutput, calls=%fused_computation.26 | convolution fusion | flops 1621753856 | bytes 7872542 | tf_op jit(solution)/shard_map/thd,hde->the/dot_general | solution.py:75
  169.5 0.0 all-gather.12.cloned.1.call-update
  169.5 4.0 %copy.41 = bf16[512,2048]{0,1:T(8,128)(2,1)} copy(bf16[512,2048]{1,0:T(8,128)(2,1)} %param.10) | data formatting | bytes 4194304 | tf_op args[4]
  173.5 39.7 %all_to_all.19 = bf16[512,4,512]{0,2,1:T(8,128)(2,1)} all-to-all(bf16[512,4,512]{0,2,1:T(8,128)(2,1)} %bitcast.51), channel_id=1, replica_groups=mesh['seq_0'=8,'seq_1'=4,'seq_2'=2,'head'=4] {'head'}, dimensions={1} | all-to-all | bytes 4194304 | tf_op jit(solution)/shard_map/all_to_all | solution.py:80
  213.2 4.2 %copy.42 = bf16[4,512,512]{2,1,0:T(8,128)(2,1)} copy(bf16[4,512,512]{1,2,0:T(8,128)(2,1)} %bitcast.50) | data formatting | bytes 4194304 | tf_op jit(solution)/shard_map/all_to_all | solution.py:80
  217.4 21.0 %all-gather.12.cloned.1.call-done = bf16[1024,2048]{0,1:T(8,128)(2,1)} async-done(((bf16[1024,512]{0,1:T(8,128)(2,1)}), bf16[1024,2048]{0,1:T(8,128)(2,1)}) %all-gather.12.cloned.1.call-update) | async-done | bytes 4194320 | tf_op jit(solution)/shard_map/all_gather | solution.py:82
  238.4 6.2 %convolution_convert_fusion = bf16[1024,512]{1,0:T(8,128)(2,1)} fusion(bf16[1024,2048]{0,1:T(8,128)(2,1)} %all-gather.12.cloned.1.call-done, bf16[2048,512]{1,0:T(8,128)(2,1)} %bitcast.52), kind=kOutput, calls=%fused_computation.29 | convolution fusion | flops 2148007936 | bytes 7340032 | tf_op jit(solution)/shard_map/dot_general | solution.py:81
  (6 shorter events, 0.1 us)
Async XLA Ops:
  6.5 57.0 %copy-start = (bf16[2048,512]{1,0:T(8,128)(2,1)S(1)}, bf16[2048,512]{1,0:T(8,128)(2,1)}, u32[]{:S(2)}) copy-start(bf16[2048,512]{1,0:T(8,128)(2,1)} %param.8) | copy-start | bytes 6291460
  6.5 57.0 %all-gather.6.cloned.1.call-start = ((), (), s32[]{:S(2)}) async-start(), calls=%async_computation.1 | async-start | bytes 5242880 | tf_op jit(solution)/shard_map/all_gather | solution.py:52
  7.3 99.6 %all-gather.8.cloned.1.call-start = ((), (), s32[]{:S(2)}) async-start(), calls=%async_computation.2 | async-start | bytes 1310720 | tf_op jit(solution)/shard_map/all_gather | solution.py:22
  72.1 5.3 %copy-start.1 = (bf16[1024,2,256]{2,0,1:T(8,128)(2,1)S(1)}, bf16[1024,2,256]{2,0,1:T(8,128)(2,1)}, u32[]{:S(2)}) copy-start(bf16[1024,2,256]{2,0,1:T(8,128)(2,1)} %copy.33) | copy-start | bytes 3145732
  77.4 1.3 copy-start.3
  77.4 4.8 %copy-start.2 = (f32[2]{0:T(128)S(1)}, f32[2]{0:T(128)}, u32[]{:S(2)}) copy-start(f32[2]{0:T(128)} %param.11) | copy-start | bytes 28
  82.1 80.0 %all-gather.10.cloned.1.call-start = ((), (), s32[]{:S(2)}) async-start(), calls=%async_computation.3 | async-start | bytes 2359296 | tf_op jit(solution)/shard_map/all_gather | solution.py:22
  108.9 129.4 %all-gather.12.cloned.1.call-start = ((), (), s32[]{:S(2)}) async-start(), calls=%async_computation.4 | async-start | bytes 5242880 | tf_op jit(solution)/shard_map/all_gather | solution.py:82
Sparse Core Ops, SparseCore 0:
  9.1 54.3 all-gather.5
  82.2 24.5 all-gather.7
  109.0 39.1 all-gather.9
  169.6 68.6 all-gather.11
where the time goes:
time: 252 us; the launch traced here: 251 us
  waiting for transfers between devices  103 us (41%)
  blocking collectives  68.1 us (27%)
  matrix products  50.1 us (20%)
  between operations  13.2 us (5%)
  local copies, waits for them, and re-layouts  12.8 us (5%)
  other arithmetic  4.18 us (2%)
    all_gather x1, waiting for transfers between devices, on_device(): piece = lax.all_gather(tokens, 'head', axis=1, tiled=True)  56.3 us
    all_to_all x1, blocking collectives, on_device(): lax.all_to_all(w_out, 'head', split_axis=1, concat_axis=0, tiled=True)  39.7 us
    all_gather x4, blocking collectives, carried_in(): lax.all_gather(part.astype(kind), axis)  28.4 us
    all_gather x2, waiting for transfers between devices, carried_in(): lax.all_gather(part.astype(kind), axis)  24.7 us
    all_gather x1, waiting for transfers between devices, on_device(): lax.all_gather(mixed, 'head', axis=1, tiled=True)  21 us
    dot_general x3, matrix products, on_device(): result.append(jnp.dot(piece, weight, preferred_element_type=jnp.float32))  17.7 us
    sub x1, matrix products, on_device(): expo = jnp.exp(scores - jnp.max(scores, axis=2, keepdims=True))  8.38 us
    dot_general x1, matrix products, on_device(): jnp.einsum('thd,hde->the', fquery, memory, precision=lax.Precision.HIGHEST)  7.36 us
  transfers between devices with their start and end apart: 4, of which 3 were waited for; matrix products, arithmetic and copies ran while one was open for 14% of the time, Pallas kernels for 0%

commit v1 on v0

--- a/solution.py
+++ b/solution.py
@@ -49,7 +49,9 @@
     hsize = width // heads
     empty = jnp.zeros((seg, width), jnp.float32)
     totals = (empty, empty, empty)
-    piece = lax.all_gather(tokens, "head", axis=1, tiled=True)
+    piece = jnp.concatenate(
+        lax.all_to_all(jnp.stack([tokens] * lax.axis_size("head")), "head", 0, 0), axis=1
+    )
     result = []
     for total, weight in zip(totals, (w_query, w_key, w_value)):
         result.append(jnp.dot(piece, weight, preferred_element_type=jnp.float32))

time: 252 us -> 247 us (0.980)
  waiting for transfers between devices: 103 us -> 45.9 us
  blocking collectives: 68.1 us -> 122 us
  matrix products: 50.1 us -> 46.6 us
    all_gather x1 -> x0, waiting for transfers between devices: 56.3 us -> none  [on_device(): piece = lax.all_gather(tokens, 'head', axis=1, tiled=True)]
    all_to_all x0 -> x1, blocking collectives: none -> 52.9 us  [on_device(): lax.all_to_all(jnp.stack([tokens] * lax.axis_size('head')), 'head', 0, 0)]
    dot_general x3, matrix products: 17.7 us -> 12.8 us  [on_device(): result.append(jnp.dot(piece, weight, preferred_element_type=jnp.float32))]
    unnamed x9 -> x12, local copies, waits for them, and re-layouts: 4.01 us -> 5.64 us
  transfers between devices with their start and end apart: 4 -> 3, of which waited for: 3 -> 2; matrix products, arithmetic and copies ran while one was open for 14% -> 14% of each run, Pallas kernels for 0% -> 0%
where the time goes in v1:
time: 247 us; the launch traced here: 246 us
  blocking collectives  122 us (49%)
  matrix products  46.6 us (19%)
  waiting for transfers between devices  45.9 us (19%)
  local copies, waits for them, and re-layouts  14 us (6%)
  between operations  13.2 us (5%)
  other arithmetic  4.16 us (2%)
    all_to_all x1, blocking collectives, on_device(): lax.all_to_all(jnp.stack([tokens] * lax.axis_size('head')), 'head', 0, 0)  52.9 us
    all_to_all x1, blocking collectives, on_device(): lax.all_to_all(w_out, 'head', split_axis=1, concat_axis=0, tiled=True)  40.1 us
    all_gather x4, blocking collectives, carried_in(): lax.all_gather(part.astype(kind), axis)  29.4 us
    all_gather x2, waiting for transfers between devices, carried_in(): lax.all_gather(part.astype(kind), axis)  25.3 us
    all_gather x1, waiting for transfers between devices, on_device(): lax.all_gather(mixed, 'head', axis=1, tiled=True)  20.6 us
    dot_general x3, matrix products, on_device(): result.append(jnp.dot(piece, weight, preferred_element_type=jnp.float32))  12.8 us
    sub x1, matrix products, on_device(): expo = jnp.exp(scores - jnp.max(scores, axis=2, keepdims=True))  8.39 us
    dot_general x1, matrix products, on_device(): jnp.einsum('thd,hde->the', fquery, memory, precision=lax.Precision.HIGHEST)  7.36 us
  transfers between devices with their start and end apart: 3, of which 2 were waited for; matrix products, arithmetic and copies ran while one was open for 14% of the time, Pallas kernels for 0%

profile of v1, /device:TPU:1, one launch (start us, length us, event | category | flops | bytes accessed | tf_op | source)
XLA Modules:
  0.0 246.3 jit_solution(4145251127590926697)
XLA Ops:
  6.5 0.0 copy-start
  6.5 0.0 all-gather.5.cloned.1.call-start
  6.5 1.6 copy.35
  8.2 0.5 stack.2
  8.7 0.0 copy-start.3
  8.7 52.9 %all_to_all.24 = bf16[4,1024,512]{1,2,0:T(8,128)(2,1)S(1)} all-to-all(bf16[4,1024,512]{1,2,0:T(8,128)(2,1)S(1)} %stack.2), channel_id=1, replica_groups=mesh['seq_0'=8,'seq_1'=4,'seq_2'=2,'head'=4] {'head'}, dimensions={0} | all-to-all | bytes 8388608 | tf_op jit(solution)/shard_map/all_to_all | solution.py:53
  61.6 0.0 copy-start.1
  61.6 0.0 copy-done.3
  61.6 3.4 %convolution_convert_fusion.2 = bf16[1024,512]{0,1:T(8,128)(2,1)} fusion(bf16[1024,2048]{0,1:T(8,128)(2,1)S(1)} %bitcast.55, bf16[2048,512]{1,0:T(8,128)(2,1)S(1)} %copy-done.3), kind=kOutput, calls=%fused_computation.31 | convolution fusion | flops 2148007936 | bytes 7340032 | tf_op jit(solution)/shard_map/dot_general | solution.py:57
  65.0 0.0 copy-done.1
  65.0 0.0 copy-done
  65.0 3.2 %fusion.20 = (bf16[512]{0:T(512)(128)(2,1)S(1)}, bf16[1024,512]{0,1:T(8,128)(2,1)S(1)}) fusion(bf16[1024,2048]{0,1:T(8,128)(2,1)S(1)} %bitcast.56, bf16[2048,512]{1,0:T(8,128)(2,1)S(1)} %copy-done), kind=kOutput, calls=%fused_computation.36 | convolution fusion | flops 2151677440 | bytes 7341056 | tf_op jit(solution)/shard_map/dot_general | solution.py:57
  68.2 0.0 copy-start.2
  68.2 1.4 copy.36
  69.5 0.0 copy-done.2
  69.5 0.0 copy-start.4
  69.5 2.8 %convolution_convert_fusion.4 = bf16[2,256,256]{2,1,0:T(8,128)(2,1)S(1)} fusion(bf16[1024,2,256]{0,2,1:T(8,128)(2,1)} %bitcast.64, bf16[1024,2,256]{2,0,1:T(8,128)(2,1)} %copy.36), kind=kOutput, calls=%fused_computation.33 | convolution fusion | flops 271712256 | bytes 2359296 | tf_op jit(solution)/shard_map/thd,the->hde/dot_general | solution.py:63
  72.3 3.6 %all-gather = bf16[4,256,256]{2,1,0:T(8,128)(2,1)S(1)} all-gather(bf16[2,256,256]{2,1,0:T(8,128)(2,1)S(1)} %convolution_convert_fusion.4), channel_id=2, replica_groups=mesh['seq_0'=8,'seq_1'=4,'seq_2'=2,'head'=4] {'seq_2'}, dimensions={0}, use_global_device_ids=true | all-gather | bytes 786432 | tf_op jit(solution)/shard_map/all_gather | solution.py:22
  76.0 0.8 fusion.59
  76.7 0.0 all-gather.5.cloned.1.call-update
  76.8 0.0 all-gather.7.cloned.1.call-start
  76.8 0.0 copy-done.4
  76.8 25.3 %all-gather.5.cloned.1.call-done = bf16[4,2,256,256]{3,2,1,0:T(8,128)(2,1)} async-done(((bf16[1,2,256,256]{3,2,1,0:T(8,128)(2,1)}), bf16[4,2,256,256]{3,2,1,0:T(8,128)(2,1)}) %all-gather.5.cloned.1.call-update) | async-done | bytes 1048592 | tf_op jit(solution)/shard_map/all_gather | solution.py:22
  102.1 2.0 fusion.55
  104.1 0.0 all-gather.7.cloned.1.call-update
  104.2 0.0 all-gather.9.cloned.1.call-start
  104.2 1.3 iota_compare_fusion
  105.5 6.2 %convolution_convert_fusion.1 = bf16[1024,512]{0,1:T(8,128)(2,1)} fusion(bf16[1024,2048]{0,1:T(8,128)(2,1)} %bitcast.57, bf16[2048,512]{1,0:T(8,128)(2,1)} %param.7), kind=kOutput, calls=%fused_computation.30 | convolution fusion | flops 2148007936 | bytes 7340032 | tf_op jit(solution)/shard_map/dot_general | solution.py:57
  111.7 2.2 copy.39
  114.0 4.2 %all_gather.36 = bf16[2,2,256]{2,1,0:T(2,128)(2,1)S(1)} all-gather(bf16[1,2,256]{2,1,0:T(2,128)(2,1)S(1)} %all_gather.35), channel_id=1, replica_groups=mesh['seq_0'=8,'seq_1'=4,'seq_2'=2,'head'=4] {'seq_2'}, dimensions={0}, use_global_device_ids=true | all-gather | bytes 3072 | tf_op jit(solution)/shard_map/all_gather | solution.py:22
  118.2 6.7 %all_gather.37 = bf16[4,2,256]{2,1,0:T(2,128)(2,1)S(1)} all-gather(bf16[1,2,256]{2,1,0:T(2,128)(2,1)S(1)} %fusion.106), channel_id=1, replica_groups=mesh['seq_0'=8,'seq_1'=4,'seq_2'=2,'head'=4] {'seq_1'}, dimensions={0}, use_global_device_ids=true | all-gather | bytes 5120 | tf_op jit(solution)/shard_map/all_gather | solution.py:22
  124.9 14.9 %all_gather.38 = bf16[8,2,256]{2,1,0:T(2,128)(2,1)S(1)} all-gather(bf16[1,2,256]{2,1,0:T(2,128)(2,1)S(1)} %fusion.105), channel_id=1, replica_groups=mesh['seq_0'=8,'seq_1'=4,'seq_2'=2,'head'=4] {'seq_0'}, dimensions={0}, use_global_device_ids=true | all-gather | bytes 9216 | tf_op jit(solution)/shard_map/all_gather | solution.py:22
  139.8 2.8 %fusion.56 = f32[2,1,1024]{2,1,0:T(1,128)S(1)} fusion(bf16[1024,2,256]{2,0,1:T(8,128)(2,1)} %copy.39, f32[2,256,1]{1,0,2:T(2,128)S(1)} %fusion.94), kind=kOutput, calls=%fused_computation.76 | convolution fusion | flops 9437184 | bytes 1058816 | tf_op jit(solution)/shard_map/thd,hd->th/dot_general | solution.py:78
  142.6 8.4 %fusion.115 = (f32[2,1024]{1,0:T(2,128)S(1)}, f32[2,1024,1024]{1,2,0:T(8,128)}) fusion(pred[1024,1024]{0,1:T(8,128)(4,1)} %iota_compare_fusion, bf16[1024,2,256]{0,2,1:T(8,128)(2,1)} %bitcast.63, bf16[1024,2,256]{0,2,1:T(8,128)(2,1)} %bitcast.60), kind=kOutput, calls=%fused_computation.145 | convolution fusion | flops 1082131456 | bytes 11542528 | tf_op jit(solution)/shard_map/sub | solution.py:73
  151.0 6.3 %fusion.4 = f32[2,256,1024]{2,1,0:T(8,128)} fusion(bf16[1024,2,256]{0,2,1:T(8,128)(2,1)} %bitcast.65, f32[2,1024,1024]{1,2,0:T(8,128)} %get-tuple-element.8, f32[2,1024]{1,0:T(2,128)S(1)} %get-tuple-element.7), kind=kOutput, calls=%fused_computation.14 | convolution fusion | flops 1077936128 | bytes 11542528 | tf_op jit(solution)/shard_map/hqk,khd->qhd/dot_general | solution.py:75
  157.3 0.0 all-gather.7.cloned.1.call-done
  157.3 7.4 %fusion.15 = bf16[1024,2,256]{0,2,1:T(8,128)(2,1)} fusion(f32[2,256,1024]{2,1,0:T(8,128)} %fusion.4, f32[2]{0:T(128)S(1)} %get-tuple-element.5, f32[1024,2]{0,1:T(2,128)S(1)} %fusion.90, f32[2]{0:T(128)S(1)} %get-tuple-element.6, bf16[1024,2,256]{2,0,1:T(8,128)(2,1)} %copy.39, bf16[8,2,256,256]{3,2,1,0:T(8,128)(2,1)} %all-gather.7.cloned.1.call-done, ...), kind=kOutput, calls=%fused_computation.26 | convolution fusion | flops 1621753856 | bytes 7872542 | tf_op jit(solution)/shard_map/thd,hde->the/dot_general | solution.py:77
  164.7 0.0 all-gather.9.cloned.1.call-update
  164.7 4.0 %copy.44 = bf16[512,2048]{0,1:T(8,128)(2,1)} copy(bf16[512,2048]{1,0:T(8,128)(2,1)} %param.10) | data formatting | bytes 4194304 | tf_op args[4]
  168.7 40.1 %all_to_all.25 = bf16[512,4,512]{0,2,1:T(8,128)(2,1)} all-to-all(bf16[512,4,512]{0,2,1:T(8,128)(2,1)} %bitcast.54), channel_id=1, replica_groups=mesh['seq_0'=8,'seq_1'=4,'seq_2'=2,'head'=4] {'head'}, dimensions={1} | all-to-all | bytes 4194304 | tf_op jit(solution)/shard_map/all_to_all | solution.py:82
  208.8 4.2 %copy.45 = bf16[4,512,512]{2,1,0:T(8,128)(2,1)} copy(bf16[4,512,512]{1,2,0:T(8,128)(2,1)} %bitcast.53) | data formatting | bytes 4194304 | tf_op jit(solution)/shard_map/all_to_all | solution.py:82
  213.0 20.6 %all-gather.9.cloned.1.call-done = bf16[1024,2048]{0,1:T(8,128)(2,1)} async-done(((bf16[1024,512]{0,1:T(8,128)(2,1)}), bf16[1024,2048]{0,1:T(8,128)(2,1)}) %all-gather.9.cloned.1.call-update) | async-done | bytes 4194320 | tf_op jit(solution)/shard_map/all_gather | solution.py:84
  233.6 6.2 %convolution_convert_fusion = bf16[1024,512]{1,0:T(8,128)(2,1)} fusion(bf16[1024,2048]{0,1:T(8,128)(2,1)} %all-gather.9.cloned.1.call-done, bf16[2048,512]{1,0:T(8,128)(2,1)} %bitcast.58), kind=kOutput, calls=%fused_computation.29 | convolution fusion | flops 2148007936 | bytes 7340032 | tf_op jit(solution)/shard_map/dot_general | solution.py:83
  (6 shorter events, 0.1 us)
Async XLA Ops:
  6.5 58.5 %copy-start = (bf16[2048,512]{1,0:T(8,128)(2,1)S(1)}, bf16[2048,512]{1,0:T(8,128)(2,1)}, u32[]{:S(2)}) copy-start(bf16[2048,512]{1,0:T(8,128)(2,1)} %param.8) | copy-start | bytes 6291460
  6.5 95.6 %all-gather.5.cloned.1.call-start = ((), (), s32[]{:S(2)}) async-start(), calls=%async_computation.2 | async-start | bytes 1310720 | tf_op jit(solution)/shard_map/all_gather | solution.py:22
  8.7 52.9 %copy-start.3 = (bf16[2048,512]{1,0:T(8,128)(2,1)S(1)}, bf16[2048,512]{1,0:T(8,128)(2,1)}, u32[]{:S(2)}) copy-start(bf16[2048,512]{1,0:T(8,128)(2,1)} %param.9) | copy-start | bytes 6291460
  61.6 3.4 %copy-start.1 = (bf16[4,1024,512]{1,2,0:T(8,128)(2,1)}, bf16[4,1024,512]{1,2,0:T(8,128)(2,1)S(1)}, u32[]{:S(2)}) copy-start(bf16[4,1024,512]{1,2,0:T(8,128)(2,1)S(1)} %all_to_all.24) | copy-start | bytes 12582916
  68.2 1.4 copy-start.2
  69.5 7.3 %copy-start.4 = (f32[2]{0:T(128)S(1)}, f32[2]{0:T(128)}, u32[]{:S(2)}) copy-start(f32[2]{0:T(128)} %param.11) | copy-start | bytes 28
  76.8 80.6 %all-gather.7.cloned.1.call-start = ((), (), s32[]{:S(2)}) async-start(), calls=%async_computation.3 | async-start | bytes 2359296 | tf_op jit(solution)/shard_map/all_gather | solution.py:22
  104.2 129.4 %all-gather.9.cloned.1.call-start = ((), (), s32[]{:S(2)}) async-start(), calls=%async_computation.4 | async-start | bytes 5242880 | tf_op jit(solution)/shard_map/all_gather | solution.py:84
Sparse Core Ops, SparseCore 0:
  76.9 25.1 all-gather.4
  104.3 39.1 all-gather.6
  164.8 68.6 all-gather.8
